TPU v7x, 16 devices: a 4x2x1 block of a 4x4x8 slice. The times are simulated.
16 devices in a mesh: dp: 2 (over y, z), tp: 8 (over x, core).
Axes of the slice: x: 4, y: 2, z: 1, core: 2. Of those that a mesh axis runs over, the one named last changes fastest.
The devices are a block of a 4x4x8 slice.
Arguments:
- hidden: bfloat16 [12, 384, 5120], P('dp', 'tp'), parts along dimension 0
- lengths: int32 [12], P('dp'), parts along dimension 0
- rope_cos: float32 [12, 384, 32], P('dp'), parts along dimension 0
- rope_sin: float32 [12, 384, 32], P('dp'), parts along dimension 0
- cache_lat: bfloat16 [12, 896, 512], P('dp'), parts along dimension 0
- cache_pe: bfloat16 [12, 896, 64], P('dp'), parts along dimension 0
- norm_in: float32 [5120], replicated
- w_dq: bfloat16 [5120, 1536], replicated
- norm_q: float32 [1536], replicated
- w_dkv: bfloat16 [5120, 576], replicated
- norm_kv: float32 [512], replicated
- w_uq: bfloat16 [1536, 128, 192], P(None, 'tp')
- w_uk: bfloat16 [512, 128, 128], P(None, 'tp')
- w_uv: bfloat16 [512, 128, 128], P(None, 'tp')
- w_out: bfloat16 [16384, 5120], P('tp')
Outputs:
- output 1: bfloat16 [12, 384, 5120], P('dp', 'tp'), parts along dimension 0
- output 2: bfloat16 [12, 896, 512], P('dp'), parts along dimension 0
- output 3: bfloat16 [12, 896, 64], P('dp'), parts along dimension 0
There are 2 independent parts. A program takes and returns all parts, laid end to end along the dimension named above; an argument that names none is the same for every part.
All inputs are finite; a program needn't handle non-finite values.
Results may differ from a plain program's by a relative error of at most 0.0145318.
Values are sent between devices in bfloat16 or wider.
A program may use at most 768 MiB of HBM per device.

v0:
```python
import jax
import jax.numpy as jnp
from jax import lax
from jax.sharding import PartitionSpec as P


def rms_norm(values, gain_vec):
    inv_rms = lax.rsqrt(jnp.mean(values * values, axis=-1, keepdims=True) + 1e-6)
    return values * inv_rms * gain_vec


def apply_rope(values, cos_tab, sin_tab):
    half_dim = values.shape[-1] // 2
    lower_half = values[..., :half_dim]
    upper_half = values[..., half_dim:]
    return jnp.concatenate([lower_half * cos_tab - upper_half * sin_tab, upper_half * cos_tab + lower_half * sin_tab], axis=-1)


def write_rows(old_rows, new_rows, start_row):
    return lax.dynamic_update_slice(old_rows, new_rows, (start_row, 0))


def solution(mesh):
    def local_step(hidden, lengths, rope_cos, rope_sin, cache_lat, cache_pe, norm_in, w_dq, norm_q, w_dkv, norm_kv, w_uq, w_uk, w_uv, w_out):
        gathered = lax.all_gather(hidden, "tp", axis=1, tiled=True)
        chunk_len = gathered.shape[1]
        model_dim = gathered.shape[2]
        kv_rank, heads_local, nope_dim = w_uk.shape
        value_dim = w_uv.shape[2]
        rope_dim = cache_pe.shape[2]
        cache_len = cache_lat.shape[1]
        normed = rms_norm(gathered.astype(jnp.float32), norm_in).astype(jnp.bfloat16)
        q_latent = rms_norm(jnp.einsum("btd,dq->btq", normed, w_dq, preferred_element_type=jnp.float32), norm_q).astype(jnp.bfloat16)
        kv_proj = jnp.einsum("btd,dk->btk", normed, w_dkv, preferred_element_type=jnp.float32)
        new_lat = rms_norm(kv_proj[..., :kv_rank], norm_kv).astype(jnp.bfloat16)
        new_pe = apply_rope(kv_proj[..., kv_rank:], rope_cos, rope_sin).astype(jnp.bfloat16)
        lat_all = jax.vmap(write_rows)(cache_lat, new_lat, lengths)
        pe_all = jax.vmap(write_rows)(cache_pe, new_pe, lengths)
        q_full = jnp.einsum("btq,qhd->bthd", q_latent, w_uq, preferred_element_type=jnp.float32)
        q_nope = q_full[..., :nope_dim].astype(jnp.bfloat16)
        q_pe = apply_rope(q_full[..., nope_dim:], rope_cos[:, :, None, :], rope_sin[:, :, None, :]).astype(jnp.bfloat16)
        keys_nope = jnp.einsum("bsc,chd->bshd", lat_all, w_uk, preferred_element_type=jnp.float32).astype(jnp.bfloat16)
        values_all = jnp.einsum("bsc,chv->bshv", lat_all, w_uv, preferred_element_type=jnp.float32).astype(jnp.bfloat16)
        scores = jnp.einsum("bthd,bshd->bhts", q_nope, keys_nope, preferred_element_type=jnp.float32)
        scores = scores + jnp.einsum("bthr,bsr->bhts", q_pe, pe_all, preferred_element_type=jnp.float32)
        key_pos = jnp.arange(cache_len)[None, None, :]
        row_limit = lengths[:, None, None] + jnp.arange(chunk_len)[None, :, None] + 1
        visible = (key_pos < row_limit)[:, None, :, :]
        scores = jnp.where(visible, scores * ((nope_dim + rope_dim) ** -0.5), -1e30)
        attn_probs = jax.nn.softmax(scores, axis=-1).astype(jnp.bfloat16)
        attn_out = jnp.einsum("bhts,bshv->bthv", attn_probs, values_all, preferred_element_type=jnp.float32).astype(jnp.bfloat16)
        out_heads = w_out.reshape(heads_local, value_dim, model_dim)
        head_sum = jnp.einsum("bthv,hvd->btd", attn_out, out_heads, preferred_element_type=jnp.float32)
        reduced = lax.psum_scatter(head_sum, "tp", scatter_dimension=1, tiled=True)
        return (reduced + hidden.astype(jnp.float32)).astype(jnp.bfloat16), lat_all, pe_all

    spec_tok = P("dp", "tp", None)
    spec_len = P("dp")
    spec_seq = P("dp", None, None)
    spec_vec = P(None)
    spec_mat = P(None, None)
    spec_head = P(None, "tp", None)
    spec_rows = P("tp", None)
    in_specs = (spec_tok, spec_len, spec_seq, spec_seq, spec_seq, spec_seq, spec_vec, spec_mat, spec_vec, spec_mat, spec_vec, spec_head, spec_head, spec_head, spec_rows)
    return jax.shard_map(local_step, mesh=mesh, in_specs=in_specs, out_specs=(spec_tok, spec_seq, spec_seq), check_vma=False)
```

profile of v0, /device:TPU:112, one launch (start us, length us, event | category | flops | bytes accessed | tf_op | source)
XLA Modules:
  0.0 954.4 jit_solution(8750389590091694416)
XLA Ops:
  7.3 5.8 copy.63
  13.4 2.3 iota_compare_fusion
  15.8 110.5 %all-gather.2.cloned.1.call-done = bf16[6,384,5120]{2,1,0:T(8,128)(2,1)} async-done(((bf16[6,48,5120]{2,1,0:T(8,128)(2,1)}), bf16[6,384,5120]{2,1,0:T(8,128)(2,1)}) %all-gather.2.cloned.1.call-update) | async-done | bytes 23592976 | tf_op jit(solution)/shard_map/all_gather | solution.py:25
  126.2 9.9 %fusion.4 = f32[6,384]{1,0:T(8,128)S(1)} fusion(bf16[6,384,5120]{2,1,0:T(8,128)(2,1)} %all-gather.2.cloned.1.call-done), kind=kLoop, calls=%fused_computation.16 | loop fusion | flops 35387136 | bytes 23602176 | tf_op jit(solution)/shard_map/reduce_sum | solution.py:8
  136.2 19.6 %fusion.14 = f32[6,384,576]{1,2,0:T(8,128)S(1)} fusion(bf16[6,384,5120]{2,1,0:T(8,128)(2,1)} %all-gather.2.cloned.1.call-done, f32[5120]{0:T(1024)S(1)} %copy-done.12, f32[6,384]{1,0:T(8,128)S(1)} %add_rsqrt_fusion.2, bf16[5120,576]{0,1:T(8,128)(2,1)} %param.24), kind=kOutput, calls=%fused_computation.26 | convolution fusion | flops 13636730880 | bytes 34829312 | tf_op jit(solution)/shard_map/btd,dk->btk/dot_general | solution.py:34
  156.1 1.9 copy-done.2
  158.1 1.9 multiply_convert_fusion.1
  160.0 71.6 %while.2 = (s32[]{:T(128)}, bf16[6,896,512]{2,1,0:T(8,128)(2,1)}, s32[6,3]{0,1:T(4,128)S(1)}, bf16[6,384,512]{1,2,0:T(8,128)(2,1)}, s32[]{:T(128)}, /*index=5*/s32[3]{0:T(128)S(1)}, s32[]{:T(128)}) while((s32[]{:T(128)}, bf16[6,896,512]{2,1,0:T(8,128)(2,1)}, s32[6,3]{0,1:T(4,128)S(1)}, bf16[6,384,512]{1,2,0:T(8,128)(2,1)}, s32[]{:T(128)}, ...), condition=%wide.while_cond, body=%wide.while_body.sunk | while | flops 196627 | bytes 3539115 | solution.py:20
  160.7 2.6 and_reduce_fusion.4
  163.3 1.0 constant_dynamic-slice_fusion.6
  164.5 3.0 dynamic-slice_select_fusion.4
  167.5 4.6 dynamic-update-slice.6
  172.7 2.6 and_reduce_fusion.4
  175.4 1.0 constant_dynamic-slice_fusion.6
  176.6 3.0 dynamic-slice_select_fusion.4
  179.6 4.6 dynamic-update-slice.6
  184.8 2.6 and_reduce_fusion.4
  187.5 1.0 constant_dynamic-slice_fusion.6
  188.7 3.0 dynamic-slice_select_fusion.4
  191.7 4.3 dynamic-update-slice.6
  196.7 2.6 and_reduce_fusion.4
  199.3 1.0 constant_dynamic-slice_fusion.6
  200.5 3.0 dynamic-slice_select_fusion.4
  203.5 4.6 dynamic-update-slice.6
  208.7 2.6 and_reduce_fusion.4
  211.4 1.0 constant_dynamic-slice_fusion.6
  212.6 3.0 dynamic-slice_select_fusion.4
  215.6 4.6 dynamic-update-slice.6
  220.8 2.6 and_reduce_fusion.4
  223.5 1.0 constant_dynamic-slice_fusion.6
  224.7 3.0 dynamic-slice_select_fusion.4
  227.7 4.0 dynamic-update-slice.6
  231.7 47.2 %multiply_reduce_fusion = (f32[6,384]{1,0:T(8,128)S(1)}, f32[6,384,1536]{2,1,0:T(8,128)}) fusion(bf16[5120,1536]{1,0:T(8,128)(2,1)} %param.22, bf16[6,384,5120]{2,1,0:T(8,128)(2,1)} %all-gather.2.cloned.1.call-done, f32[5120]{0:T(1024)S(1)} %copy-done.12, f32[6,384]{1,0:T(8,128)S(1)} %add_rsqrt_fusion.2), kind=kOutput, calls=%fused_computation.30 | convolution fusion | flops 36293046272 | bytes 53516288 | tf_op jit(solution)/shard_map/btd,dq->btq/dot_general | solution.py:33
  278.9 1.2 subtract_convert_fusion.1
  280.0 0.7 pad_maximum_fusion
  280.8 49.0 %while.3 = (s32[]{:T(128)}, bf16[6,896,64]{1,2,0:T(8,128)(2,1)S(1)}, s32[6,3]{0,1:T(4,128)S(1)}, bf16[6,384,64]{1,2,0:T(8,128)(2,1)}, s32[]{:T(128)}, /*index=5*/s32[3]{0:T(128)S(1)}, s32[]{:T(128)}) while((s32[]{:T(128)}, bf16[6,896,64]{1,2,0:T(8,128)(2,1)S(1)}, s32[6,3]{0,1:T(4,128)S(1)}, bf16[6,384,64]{1,2,0:T(8,128)(2,1)}, s32[]{:T(128)}, ...), condition=%wide.while_cond.1, body=%wide.while_body.1.sunk | while | flops 24595 | bytes 245931 | solution.py:20
  281.5 2.7 and_reduce_fusion.5
  284.2 2.9 dynamic-slice_select_fusion.5
  287.0 2.0 dynamic-update-slice.7
  289.7 2.7 and_reduce_fusion.5
  292.4 2.9 dynamic-slice_select_fusion.5
  295.3 2.0 dynamic-update-slice.7
  298.0 2.7 and_reduce_fusion.5
  300.7 2.9 dynamic-slice_select_fusion.5
  303.5 1.9 dynamic-update-slice.7
  306.1 2.7 and_reduce_fusion.5
  308.8 2.9 dynamic-slice_select_fusion.5
  311.6 2.0 dynamic-update-slice.7
  314.3 2.7 and_reduce_fusion.5
  317.0 2.9 dynamic-slice_select_fusion.5
  319.9 2.0 dynamic-update-slice.7
  322.6 2.7 and_reduce_fusion.5
  325.3 2.9 dynamic-slice_select_fusion.5
  328.1 1.6 dynamic-update-slice.7
  329.8 38.0 %fusion.18 = f32[6,384,16,192]{1,3,2,0:T(8,128)} fusion(bf16[1536,16,192]{0,2,1:T(8,128)(2,1)} %param.26, f32[6,384,1536]{2,1,0:T(8,128)} %get-tuple-element.50, f32[1536]{0:T(1024)S(1)} %copy-done.13, f32[6,384]{1,0:T(8,128)S(1)} %add_rsqrt_fusion), kind=kOutput, calls=%fused_computation.32 | convolution fusion | flops 21753888768 | bytes 51919872 | tf_op jit(solution)/shard_map/btq,qhd->bthd/dot_general | solution.py:39
  367.8 6.1 subtract_convert_fusion
  373.9 55.1 %fusion.8 = f32[6,16,384,896]{3,2,1,0:T(8,128)} fusion(f32[6,384,16,192]{1,3,2,0:T(8,128)} %fusion.18, bf16[6,896,512]{2,1,0:T(8,128)(2,1)} %get-tuple-element.8, bf16[512,16,128,1]{2,1,0,3:T(8,128)(2,1)S(1)} %bitcast.86), kind=kOutput, calls=%fused_computation.21 | convolution fusion | flops 19741016064 | bytes 149159936 | tf_op jit(solution)/shard_map/bthd,bshd->bhts/dot_general | solution.py:44
  429.0 19.0 %fusion.28 = bf16[6,896,16,128]{3,1,2,0:T(8,128)(2,1)} fusion(bf16[6,896,512]{2,1,0:T(8,128)(2,1)} %get-tuple-element.8, bf16[512,16,128,1]{2,1,0,3:T(8,128)(2,1)} %bitcast.88), kind=kOutput, calls=%fused_computation.42 | convolution fusion | flops 11274289152 | bytes 29622272 | tf_op jit(solution)/shard_map/bsc,chv->bshv/dot_general | solution.py:43
  448.0 50.2 %copy.40 = bf16[6,896,16,128]{3,2,1,0:T(8,128)(2,1)} copy(bf16[6,896,16,128]{3,1,2,0:T(8,128)(2,1)} %fusion.28) | data formatting | bytes 44040192 | tf_op jit(solution)/shard_map/bsc,chv->bshv/dot_general | solution.py:43
  498.2 101.6 %fusion.41 = (f32[6,16,384]{2,1,0:T(8,128)S(1)}, f32[6,16,384,896]{3,2,1,0:T(8,128)}) fusion(f32[6,16,384,896]{3,2,1,0:T(8,128)} %fusion.8, pred[6,384,896]{2,1,0:T(8,128)(4,1)S(1)} %copy-done.3, bf16[6,384,16,32]{1,3,2,0:T(8,128)(2,1)} %get-tuple-element.46, bf16[6,384,16,32]{1,3,2,0:T(8,128)(2,1)} %get-tuple-element.45, ...), kind=kOutput, calls=%fused_computation.68 | convolution fusion | flops 4402447360 | bytes 271859712 | tf_op jit(solution)/shard_map/sub | solution.py:50
  599.8 52.8 %fusion.3 = bf16[6,16,128,384]{2,3,1,0:T(8,128)(2,1)} fusion(f32[6,16,384,896]{3,2,1,0:T(8,128)} %get-tuple-element.52, f32[6,16,384]{2,1,0:T(8,128)S(1)} %get-tuple-element.51, bf16[6,896,16,128]{3,2,1,0:T(8,128)(2,1)} %copy.40), kind=kOutput, calls=%fused_computation.13 | convolution fusion | flops 8521777152 | bytes 163725312 | tf_op jit(solution)/shard_map/bhts,bshv->bthv/dot_general | solution.py:51
  652.6 56.9 %convolution_bitcast_fusion = f32[6,384,5120]{2,1,0:T(8,128)} fusion(bf16[16,128,5120,1]{2,1,0,3:T(8,128)(2,1)} %bitcast.87, bf16[6,16,128,384]{2,3,1,0:T(8,128)(2,1)} %fusion.3), kind=kOutput, calls=%fused_computation.27 | convolution fusion | flops 48318382080 | bytes 77594624 | tf_op jit(solution)/shard_map/bthv,hvd->btd/dot_general | solution.py:53
  709.7 231.4 %reduce-scatter.2.cloned.1.call-done = f32[6,48,5120]{2,1,0:T(8,128)} async-done(((f32[6,384,5120]{2,1,0:T(8,128)}), f32[6,48,5120]{2,1,0:T(8,128)}) %reduce-scatter.2.cloned.1.call-update) | async-done | bytes 5898256 | tf_op jit(solution)/shard_map/reduce_scatter | solution.py:54
  941.1 6.0 add_convert_fusion
  (70 shorter events, 9.8 us)
Async XLA Ops:
  7.2 366.7 %copy-start = (bf16[512,16,128]{2,1,0:T(8,128)(2,1)S(1)}, bf16[512,16,128]{2,1,0:T(8,128)(2,1)}, u32[]{:S(2)}) copy-start(bf16[512,16,128]{2,1,0:T(8,128)(2,1)} %param.27) | copy-start | bytes 6291460
  7.2 6.1 copy-start.11
  7.2 6.0 copy-start.10
  7.2 119.0 %all-gather.2.cloned.1.call-start = ((), (), s32[]{:S(2)}) async-start(), calls=%async_computation.1 | async-start | bytes 26542080 | tf_op jit(solution)/shard_map/all_gather | solution.py:25
  13.2 927.9 %reduce-scatter.2.cloned.1.call-start = ((), (), s32[]{:S(2)}) async-start(), calls=%async_computation.2 | async-start | bytes 53084160 | tf_op jit(solution)/shard_map/reduce_scatter | solution.py:54
  15.7 120.4 %copy-start.12 = (f32[5120]{0:T(1024)S(1)}, f32[5120]{0:T(1024)}, u32[]{:S(2)}) copy-start(f32[5120]{0:T(1024)} %param.21) | copy-start | bytes 61444
  136.2 21.9 %copy-start.9 = (f32[512]{0:T(512)S(1)}, f32[512]{0:T(512)}, u32[]{:S(2)}) copy-start(f32[512]{0:T(512)} %param.25) | copy-start | bytes 6148
  155.8 2.3 copy-start.2
  155.8 4.2 copy-start.8
  231.7 47.2 %copy-start.6 = (f32[6,384,32]{1,2,0:T(8,128)S(1)}, f32[6,384,32]{1,2,0:T(8,128)}, u32[]{:S(2)}) copy-start(f32[6,384,32]{1,2,0:T(8,128)} %param.18) | copy-start | bytes 884740
  231.7 47.2 %copy-start.7 = (f32[6,384,32]{1,2,0:T(8,128)S(1)}, f32[6,384,32]{1,2,0:T(8,128)}, u32[]{:S(2)}) copy-start(f32[6,384,32]{1,2,0:T(8,128)} %param.17) | copy-start | bytes 884740
  231.7 49.1 %copy-start.5 = (bf16[6,896,64]{1,2,0:T(8,128)(2,1)S(1)}, bf16[6,896,64]{1,2,0:T(8,128)(2,1)}, u32[]{:S(2)}) copy-start(bf16[6,896,64]{1,2,0:T(8,128)(2,1)} %param.20) | copy-start | bytes 2064388
  231.7 98.1 %copy-start.13 = (f32[1536]{0:T(1024)S(1)}, f32[1536]{0:T(1024)}, u32[]{:S(2)}) copy-start(f32[1536]{0:T(1024)} %param.23) | copy-start | bytes 18436
  329.8 168.4 %copy-start.4 = (bf16[6,896,64]{1,2,0:T(8,128)(2,1)}, bf16[6,896,64]{1,2,0:T(8,128)(2,1)S(1)}, u32[]{:S(2)}) copy-start(bf16[6,896,64]{1,2,0:T(8,128)(2,1)S(1)} %get-tuple-element.16) | copy-start | bytes 2064388
  448.0 50.2 %copy-start.3 = (pred[6,384,896]{2,1,0:T(8,128)(4,1)S(1)}, pred[6,384,896]{2,1,0:T(8,128)(4,1)}, u32[]{:S(2)}) copy-start(pred[6,384,896]{2,1,0:T(8,128)(4,1)} %iota_compare_fusion) | copy-start | bytes 6193156
  709.6 237.4 %copy-start.1 = (bf16[512,16,128]{2,1,0:T(8,128)(2,1)S(1)}, bf16[512,16,128]{2,1,0:T(8,128)(2,1)}, u32[]{:S(2)}) copy-start(bf16[512,16,128]{2,1,0:T(8,128)(2,1)} %param.27) | copy-start | bytes 6291460
Sparse Core Ops, SparseCore 0:
  13.3 112.8 all-gather.1
  709.8 231.2 reduce-scatter.1
where the time goes:
time: 962 us; the launch traced here: 954 us
  matrix products  390 us (41%)
  waiting for transfers between devices  342 us (36%)
  local copies, waits for them, and re-layouts  111 us (12%)
  other arithmetic  95.6 us (10%)
  between operations  14.7 us (2%)
    reduce_scatter x1, waiting for transfers between devices, local_step(): reduced = lax.psum_scatter(head_sum, 'tp', scatter_dimension=1, tiled=True)  231 us
    all_gather x1, waiting for transfers between devices, local_step(): gathered = lax.all_gather(hidden, 'tp', axis=1, tiled=True)  110 us
    sub x1, matrix products, local_step(): attn_probs = jax.nn.softmax(scores, axis=-1).astype(jnp.bfloat16)  102 us
    scatter x24, other arithmetic  67 us
    dot_general x1, matrix products, local_step(): jnp.einsum('bthv,hvd->btd', attn_out, out_heads, preferred_element_type=j...  56.9 us
    dot_general x1, matrix products, local_step(): jnp.einsum('bthd,bshd->bhts', q_nope, keys_nope, preferred_element_type=j...  55.1 us
    scatter x48, local copies, waits for them, and re-layouts  53.4 us
    dot_general x1, matrix products, local_step(): jnp.einsum('bhts,bshv->bthv', attn_probs, values_all, preferred_element_t...  52.8 us
  transfers between devices with their start and end apart: 2, of which 2 were waited for; matrix products, arithmetic and copies ran while one was open for 0% of the time, Pallas kernels for 0%

commit v1 on v0

v1 whole, which is shorter than its diff:
```python
import functools

import jax
import jax.numpy as jnp
from jax import lax
from jax.experimental import pallas as pl
from jax.experimental.pallas import tpu as pltpu
from jax.sharding import PartitionSpec as P

BF16 = jnp.bfloat16
F32 = jnp.float32
NEG = -1e30
LOG2E = 1.4426950408889634
EPS = 1e-6
QBLK = 128
CORES = 2
MAIN_ID = 0


def rms_norm(values, gain_vec):
    inv_rms = lax.rsqrt(jnp.mean(values * values, axis=-1, keepdims=True) + EPS)
    return values * inv_rms * gain_vec


def apply_rope(values, cos_tab, sin_tab):
    half_dim = values.shape[-1] // 2
    lower_half = values[..., :half_dim]
    upper_half = values[..., half_dim:]
    return jnp.concatenate([lower_half * cos_tab - upper_half * sin_tab, upper_half * cos_tab + lower_half * sin_tab], axis=-1)


def dot_nn(lhs, rhs):
    return lax.dot_general(lhs, rhs, (((1,), (0,)), ((), ())), preferred_element_type=F32)


def dot_nt(lhs, rhs):
    return lax.dot_general(lhs, rhs, (((1,), (1,)), ((), ())), preferred_element_type=F32)


def rope_pair(values, cos_tab, sin_tab, half_dim):
    lanes = values.shape[1]
    upper = pltpu.roll(values, lanes - half_dim, 1)
    lower = pltpu.roll(values, half_dim, 1)
    lane = lax.broadcasted_iota(jnp.int32, values.shape, 1)
    swapped = jnp.where(lane % (2 * half_dim) < half_dim, upper, lower)
    return values * cos_tab + swapped * sin_tab


class Dims:
    pass


def main_kernel(dm, len_ref, gath_ref, lat_ref, pe_old_ref, cos_ref, sin_ref, wuq_ref, wuk_ref, wuv_ref, wout_ref, hid_ref, out_ref,
                q_buf, lat_buf, pe_buf, cos_buf, sin_buf, wuq_buf, wuk_buf, wuv_buf, wout_buf,
                qcat, kcat, vcat, attn_buf, part_buf, xch_buf, sum_buf, hop_buf, dir_buf, fin_buf, hid_buf, y_buf,
                seq_sem, w_sem, wout_sem, hid_sem, y_sem,
                xch_send, xch_recv, hop_send, hop_recv, dir_send, dir_recv, fin_send, fin_recv,
                credit_pair, credit_left, credit_right):
    me = lax.axis_index("tp")
    chip = me // CORES
    core = me % CORES
    chips = dm.chips
    left_chip = (chip + chips - 1) % chips
    right_chip = (chip + 1) % chips
    partner = chip * CORES + (1 - core)
    left = left_chip * CORES + core
    right = right_chip * CORES + core

    barrier = pltpu.get_barrier_semaphore()
    for peer in (partner, left, right):
        pl.semaphore_signal(barrier, inc=1, device_id={"tp": peer})
    pl.semaphore_wait(barrier, 3)

    groups, gh = dm.groups, dm.group_heads
    chunks, cw, hw, tok = dm.chunks, dm.chunk_cols, dm.half_cols, dm.tok
    attn_ticks = dm.seqs * groups
    out_ticks = dm.seqs * chunks
    nope, rope, vdim, prefix, qlen = dm.nope, dm.rope, dm.vdim, dm.prefix, dm.qlen
    nslot = dm.ring_slots

    def seq_copies(b, slot):
        return (
            pltpu.make_async_copy(gath_ref.at[b, :, pl.ds(0, dm.q_rank)], q_buf.at[slot], seq_sem.at[slot, 0]),
            pltpu.make_async_copy(lat_ref.at[b, pl.ds(0, prefix)], lat_buf.at[slot, pl.ds(0, prefix)], seq_sem.at[slot, 1]),
            pltpu.make_async_copy(gath_ref.at[b, :, pl.ds(dm.q_rank, dm.kv_rank)], lat_buf.at[slot, pl.ds(prefix, qlen)], seq_sem.at[slot, 2]),
            pltpu.make_async_copy(pe_old_ref.at[b], pe_buf.at[slot, pl.ds(0, prefix)], seq_sem.at[slot, 3]),
            pltpu.make_async_copy(gath_ref.at[b, :, pl.ds(dm.q_rank + dm.kv_rank, 2 * rope)], pe_buf.at[slot, pl.ds(prefix, qlen)], seq_sem.at[slot, 4]),
            pltpu.make_async_copy(cos_ref.at[b], cos_buf.at[slot], seq_sem.at[slot, 5]),
            pltpu.make_async_copy(sin_ref.at[b], sin_buf.at[slot], seq_sem.at[slot, 6]),
        )

    def weight_copies(g, slot):
        return (
            pltpu.make_async_copy(wuq_ref.at[pl.ds(g * gh, gh), pl.ds(0, nope)], wuq_buf.at[slot, pl.ds(0, gh * nope)].reshape(gh, nope, dm.q_rank), w_sem.at[slot, 0]),
            pltpu.make_async_copy(wuq_ref.at[pl.ds(g * gh, gh), pl.ds(nope, rope)], wuq_buf.at[slot, pl.ds(gh * nope, gh * rope)].reshape(gh, rope, dm.q_rank), w_sem.at[slot, 1]),
            pltpu.make_async_copy(wuk_ref.at[:, pl.ds(g * gh * nope, gh * nope)], wuk_buf.at[slot], w_sem.at[slot, 2]),
            pltpu.make_async_copy(wuv_ref.at[:, pl.ds(g * gh * vdim, gh * vdim)], wuv_buf.at[slot], w_sem.at[slot, 3]),
        )

    def wout_copy(j, slot):
        return pltpu.make_async_copy(wout_ref.at[:, pl.ds((j % chunks) * cw, cw)], wout_buf.at[slot], wout_sem.at[slot])

    def hid_copy(j, slot):
        return pltpu.make_async_copy(hid_ref.at[j // chunks, :, pl.ds((j % chunks) * cw, cw)], hid_buf.at[slot], hid_sem.at[slot])

    def y_copy(j, slot):
        return pltpu.make_async_copy(y_buf.at[slot], out_ref.at[j // chunks, :, pl.ds((j % chunks) * cw, cw)], y_sem.at[slot])

    def xch_copy(j, t):
        slot = j % 2
        return pltpu.make_async_remote_copy(
            src_ref=part_buf.at[slot, pl.ds(pl.multiple_of((t * CORES + 1 - core) * tok, 8), tok)],
            dst_ref=xch_buf.at[slot, t],
            send_sem=xch_send.at[slot, t],
            recv_sem=xch_recv.at[slot, t],
            device_id={"tp": partner},
        )

    def toward(u):
        if u == 0:
            return (left, left_chip), (right, right_chip)
        return (right, right_chip), (left, left_chip)

    def hop_copy(j, u):
        (down, _), _ = toward(u)
        return pltpu.make_async_remote_copy(
            src_ref=sum_buf.at[j % nslot, (chip + 2) % chips, :, pl.ds(u * hw, hw)],
            dst_ref=hop_buf.at[j % nslot, u],
            send_sem=hop_send.at[j % nslot, u],
            recv_sem=hop_recv.at[j % nslot, u],
            device_id={"tp": down},
        )

    def dir_copy(j, u):
        _, (up, up_chip) = toward(u)
        return pltpu.make_async_remote_copy(
            src_ref=sum_buf.at[j % nslot, up_chip, :, pl.ds(u * hw, hw)],
            dst_ref=dir_buf.at[j % nslot, u],
            send_sem=dir_send.at[j % nslot, u],
            recv_sem=dir_recv.at[j % nslot, u],
            device_id={"tp": up},
        )

    def fin_copy(j, u):
        (down, down_chip), _ = toward(u)
        return pltpu.make_async_remote_copy(
            src_ref=sum_buf.at[j % nslot, down_chip, :, pl.ds(u * hw, hw)],
            dst_ref=fin_buf.at[j % nslot, u],
            send_sem=fin_send.at[j % nslot, u],
            recv_sem=fin_recv.at[j % nslot, u],
            device_id={"tp": down},
        )

    def attention(b, g, wslot):
        slot = b % 2
        q_lat = q_buf[slot]
        lane = lax.broadcasted_iota(jnp.int32, (qlen, 2 * rope), 1)
        q_pe = dot_nt(q_lat, wuq_buf[wslot, gh * nope:])
        for pair in range(gh // 2):
            rotated = rope_pair(q_pe[:, pair * 2 * rope:(pair + 1) * 2 * rope], cos_buf[slot], sin_buf[slot], rope // 2)
            qcat[2 * pair, :, nope:] = jnp.where(lane < rope, rotated, 0.0).astype(BF16)
            qcat[2 * pair + 1, :, nope:] = jnp.where(lane >= rope, rotated, 0.0).astype(BF16)
        q_nope = dot_nt(q_lat, wuq_buf[wslot, :gh * nope])
        for h in range(gh):
            qcat[h, :, :nope] = q_nope[:, h * nope:(h + 1) * nope].astype(BF16)
        keys = dot_nn(lat_buf[slot], wuk_buf[wslot])
        for h in range(gh):
            kcat[h, :, :nope] = keys[:, h * nope:(h + 1) * nope].astype(BF16)
        vcat[...] = dot_nn(lat_buf[slot], wuv_buf[wslot]).astype(BF16)

        length = len_ref[b]
        key_pos = lax.broadcasted_iota(jnp.int32, (1, prefix), 1)
        bias = jnp.where(key_pos < length, 0.0, NEG).astype(F32)
        row = lax.broadcasted_iota(jnp.int32, (QBLK, QBLK), 0)
        col = lax.broadcasted_iota(jnp.int32, (QBLK, QBLK), 1)
        causal = col <= row
        nblk = qlen // QBLK
        wide = prefix + (nblk - 1) * QBLK
        for h in range(gh):
            main = dot_nt(qcat[h], kcat[h, :wide])
            last = dot_nt(qcat[h, (nblk - 1) * QBLK:], kcat[h, wide:])
            for blk in range(nblk):
                rows = slice(blk * QBLK, (blk + 1) * QBLK)
                pieces = [main[rows, :prefix] + bias]
                if blk == nblk - 1:
                    pieces.append(main[rows, prefix:wide])
                    diag = last
                else:
                    if blk > 0:
                        pieces.append(main[rows, prefix:prefix + blk * QBLK])
                    diag = main[rows, prefix + blk * QBLK:prefix + (blk + 1) * QBLK]
                pieces.append(jnp.where(causal, diag, NEG))
                top = functools.reduce(jnp.maximum, [jnp.max(piece, axis=1, keepdims=True) for piece in pieces])
                total = None
                acc = None
                start = 0
                for piece in pieces:
                    prob = jnp.exp2((piece - top) * dm.exp_scale)
                    piece_sum = jnp.sum(prob, axis=1, keepdims=True)
                    width = piece.shape[1]
                    term = dot_nn(prob.astype(BF16), vcat[start:start + width, h * vdim:(h + 1) * vdim])
                    total = piece_sum if total is None else total + piece_sum
                    acc = term if acc is None else acc + term
                    start += width
                attn_buf[slot, rows, pl.ds(pl.multiple_of((g * gh + h) * vdim, 128), vdim)] = (acc / total).astype(BF16)

    for copy in seq_copies(0, 0) + weight_copies(0, 0):
        copy.start()

    def tick(i, carry):
        b = i // groups
        g = i % groups
        wslot = i % 2

        @pl.when(i + 1 < attn_ticks)
        def _():
            for copy in weight_copies((i + 1) % groups, (i + 1) % 2):
                copy.start()

        @pl.when(jnp.logical_and(g == 1, b + 1 < dm.seqs))
        def _():
            for copy in seq_copies(b + 1, (b + 1) % 2):
                copy.start()

        j_next = i + 1 - groups

        @pl.when(jnp.logical_and(j_next >= 0, j_next < out_ticks))
        def _():
            wout_copy(j_next, j_next % 2).start()

        j1 = i - groups - 1

        @pl.when(jnp.logical_and(j1 >= 0, j1 < out_ticks))
        def _():
            hid_copy(j1, j1 % nslot).start()
            for t in range(chips):
                xch_copy(j1, t).wait_recv()
            for off in (2, 1, 3, 0):
                t = (chip + off) % chips
                rows = pl.ds(pl.multiple_of((t * CORES + core) * tok, 8), tok)
                sum_buf[j1 % nslot, t] = part_buf[j1 % 2, rows] + xch_buf[j1 % 2, t]

            @pl.when(j1 + 2 < out_ticks)
            def _():
                pl.semaphore_signal(credit_pair, inc=1, device_id={"tp": partner})

            @pl.when(j1 >= nslot)
            def _():
                pl.semaphore_wait(credit_left, 1)
                pl.semaphore_wait(credit_right, 1)

            for u in range(2):
                hop_copy(j1, u).start()
            for u in range(2):
                dir_copy(j1, u).start()

        j2 = i - groups - 2

        @pl.when(jnp.logical_and(j2 >= 0, j2 < out_ticks))
        def _():
            for u in range(2):
                hop_copy(j2, u).wait_recv()
            for u in range(2):
                _, down_chip = toward(u)[0]
                cols = pl.ds(u * hw, hw)
                sum_buf[j2 % nslot, down_chip, :, cols] = sum_buf[j2 % nslot, down_chip, :, cols] + hop_buf[j2 % nslot, u]
            for u in range(2):
                fin_copy(j2, u).start()

        j3 = i - groups - 3

        @pl.when(jnp.logical_and(j3 >= 0, j3 < out_ticks))
        def _():
            s3 = j3 % nslot
            hid_copy(j3, s3).wait()

            @pl.when(j3 >= 2)
            def _():
                y_copy(j3 - 2, j3 % 2).wait()

            for u in range(2):
                dir_copy(j3, u).wait()
                fin_copy(j3, u).wait()
                hop_copy(j3, u).wait_send()
            for u in range(2):
                cols = pl.ds(u * hw, hw)
                total = sum_buf[s3, chip, :, cols] + dir_buf[s3, u] + fin_buf[s3, u]
                y_buf[j3 % 2, :, cols] = (total + hid_buf[s3, :, cols].astype(F32)).astype(BF16)

            @pl.when(j3 + nslot < out_ticks)
            def _():
                pl.semaphore_signal(credit_left, inc=1, device_id={"tp": right})
                pl.semaphore_signal(credit_right, inc=1, device_id={"tp": left})

            y_copy(j3, j3 % 2).start()

        j0 = i - groups

        @pl.when(jnp.logical_and(j0 >= 0, j0 < out_ticks))
        def _():
            pslot = j0 % 2

            @pl.when(j0 >= 2)
            def _():
                for t in range(chips):
                    xch_copy(j0 - 2, t).wait_send()

            wout_copy(j0, pslot).wait()
            part_buf[pslot] = dot_nn(attn_buf[(j0 // chunks) % 2], wout_buf[pslot])

            @pl.when(j0 >= 2)
            def _():
                pl.semaphore_wait(credit_pair, 1)

            for t in range(chips):
                xch_copy(j0, t).start()

        @pl.when(i < attn_ticks)
        def _():
            @pl.when(g == 0)
            def _():
                for copy in seq_copies(b, b % 2):
                    copy.wait()
                for h in range(gh):
                    kcat[h, :, nope:] = pe_buf[b % 2]

            for copy in weight_copies(g, wslot):
                copy.wait()
            attention(b, g, wslot)

        return carry

    lax.fori_loop(0, out_ticks + groups + 3, tick, 0)

    for j in (out_ticks - 2, out_ticks - 1):
        for t in range(chips):
            xch_copy(j, t).wait_send()
        y_copy(j, j % 2).wait()


def attention_block(lengths, gathered, cache_lat, pe_old, cos_tab, sin_tab, w_uq_t, w_uk, w_uv, w_out, hidden, tp):
    dm = Dims()
    dm.seqs, dm.tok, dm.model = hidden.shape
    heads, head_dim, dm.q_rank = w_uq_t.shape
    dm.kv_rank = w_uk.shape[0]
    dm.nope = w_uk.shape[1] // heads
    dm.vdim = w_uv.shape[1] // heads
    dm.rope = head_dim - dm.nope
    dm.qlen = gathered.shape[1]
    dm.prefix = cache_lat.shape[1] - dm.qlen
    dm.chips = tp // CORES
    dm.group_heads = 4
    dm.groups = heads // dm.group_heads
    dm.chunks = 4
    dm.chunk_cols = dm.model // dm.chunks
    dm.half_cols = dm.chunk_cols // 2
    dm.ring_slots = 4
    dm.exp_scale = head_dim ** -0.5 * LOG2E
    gh, keys, ns = dm.group_heads, dm.prefix + dm.qlen, dm.ring_slots
    assert dm.chips == 4 and dm.groups == dm.chunks

    def vmem(*shape, dtype=BF16):
        return pltpu.VMEM(shape, dtype)

    dma = pltpu.SemaphoreType.DMA
    scratch = [
        vmem(2, dm.qlen, dm.q_rank),
        vmem(2, keys, dm.kv_rank),
        vmem(2, keys, 2 * dm.rope),
        vmem(2, dm.qlen, 2 * dm.rope, dtype=F32),
        vmem(2, dm.qlen, 2 * dm.rope, dtype=F32),
        vmem(2, gh * head_dim, dm.q_rank),
        vmem(2, dm.kv_rank, gh * dm.nope),
        vmem(2, dm.kv_rank, gh * dm.vdim),
        vmem(2, heads * dm.vdim, dm.chunk_cols),
        vmem(gh, dm.qlen, dm.nope + 2 * dm.rope),
        vmem(gh, keys, dm.nope + 2 * dm.rope),
        vmem(keys, gh * dm.vdim),
        vmem(2, dm.qlen, heads * dm.vdim),
        vmem(2, dm.qlen, dm.chunk_cols, dtype=F32),
        vmem(2, dm.chips, dm.tok, dm.chunk_cols, dtype=F32),
        vmem(ns, dm.chips, dm.tok, dm.chunk_cols, dtype=F32),
        vmem(ns, 2, dm.tok, dm.half_cols, dtype=F32),
        vmem(ns, 2, dm.tok, dm.half_cols, dtype=F32),
        vmem(ns, 2, dm.tok, dm.half_cols, dtype=F32),
        vmem(ns, dm.tok, dm.chunk_cols),
        vmem(2, dm.tok, dm.chunk_cols),
        dma((2, 7)), dma((2, 4)), dma((2,)), dma((ns,)), dma((2,)),
        dma((2, dm.chips)), dma((2, dm.chips)),
        dma((ns, 2)), dma((ns, 2)), dma((ns, 2)), dma((ns, 2)), dma((ns, 2)), dma((ns, 2)),
        pltpu.SemaphoreType.REGULAR, pltpu.SemaphoreType.REGULAR, pltpu.SemaphoreType.REGULAR,
    ]
    hbm = pl.BlockSpec(memory_space=pl.ANY)
    return pl.pallas_call(
        functools.partial(main_kernel, dm),
        out_shape=jax.ShapeDtypeStruct(hidden.shape, BF16),
        in_specs=[pl.BlockSpec(memory_space=pltpu.SMEM)] + [hbm] * 10,
        out_specs=hbm,
        scratch_shapes=scratch,
        compiler_params=pltpu.CompilerParams(collective_id=MAIN_ID, has_side_effects=True, vmem_limit_bytes=66_000_000),
        name="attend_project",
    )(lengths, gathered, cache_lat, pe_old, cos_tab, sin_tab, w_uq_t, w_uk, w_uv, w_out, hidden)


def solution(mesh):
    tp = mesh.shape["tp"]

    def local_step(hidden, lengths, rope_cos, rope_sin, cache_lat, cache_pe, norm_in, w_dq, norm_q, w_dkv, norm_kv, w_uq, w_uk, w_uv, w_out):
        seqs, tok, model = hidden.shape
        qlen = tok * tp
        kv_rank, heads, nope = w_uk.shape
        q_rank = w_dq.shape[1]
        rope = cache_pe.shape[2]
        cache_len = cache_lat.shape[1]
        prefix = cache_len - qlen
        me = lax.axis_index("tp")
        normed = rms_norm(hidden.astype(F32), norm_in).astype(BF16)
        q_latent = rms_norm(jnp.einsum("btd,dq->btq", normed, w_dq, preferred_element_type=F32), norm_q).astype(BF16)
        kv_proj = jnp.einsum("btd,dk->btk", normed, w_dkv, preferred_element_type=F32)
        new_lat = rms_norm(kv_proj[..., :kv_rank], norm_kv).astype(BF16)
        cos_own = lax.dynamic_slice_in_dim(rope_cos, me * tok, tok, axis=1)
        sin_own = lax.dynamic_slice_in_dim(rope_sin, me * tok, tok, axis=1)
        new_pe = apply_rope(kv_proj[..., kv_rank:], cos_own, sin_own).astype(BF16)
        packed = jnp.concatenate([q_latent, new_lat, new_pe, new_pe], axis=-1)
        gathered = lax.all_gather(packed, "tp", axis=1, tiled=True)
        lat_new = gathered[..., q_rank:q_rank + kv_rank]
        pe_new = gathered[..., q_rank + kv_rank:q_rank + kv_rank + rope]
        shift = jnp.arange(cache_len)[None, :] - lengths[:, None]
        pick = (shift[:, :, None] == jnp.arange(qlen)[None, None, :]).astype(BF16)
        inside = jnp.logical_and(shift >= 0, shift < qlen)[:, :, None]
        lat_all = jnp.where(inside, jnp.einsum("bti,bic->btc", pick, lat_new, preferred_element_type=F32).astype(BF16), cache_lat)
        pe_all = jnp.where(inside, jnp.einsum("bti,bic->btc", pick, pe_new, preferred_element_type=F32).astype(BF16), cache_pe)

        pe_old = jnp.concatenate([cache_pe[:, :prefix], cache_pe[:, :prefix]], axis=-1)
        cos_tab = jnp.concatenate([rope_cos] * 4, axis=-1)
        sin_tab = jnp.concatenate([-rope_sin, rope_sin] * 2, axis=-1)
        w_uq_t = jnp.transpose(w_uq, (1, 2, 0))
        block_out = attention_block(lengths, gathered, cache_lat, pe_old, cos_tab, sin_tab, w_uq_t,
                                    w_uk.reshape(kv_rank, heads * nope), w_uv.reshape(kv_rank, -1), w_out, hidden, tp)
        return block_out, lat_all, pe_all

    spec_tok = P("dp", "tp", None)
    spec_len = P("dp")
    spec_seq = P("dp", None, None)
    spec_vec = P(None)
    spec_mat = P(None, None)
    spec_head = P(None, "tp", None)
    spec_rows = P("tp", None)
    in_specs = (spec_tok, spec_len, spec_seq, spec_seq, spec_seq, spec_seq, spec_vec, spec_mat, spec_vec, spec_mat, spec_vec, spec_head, spec_head, spec_head, spec_rows)
    return jax.shard_map(local_step, mesh=mesh, in_specs=in_specs, out_specs=(spec_tok, spec_seq, spec_seq), check_vma=False)
```

time: 962 us -> 336 us (0.35)
  matrix products: 390 us -> 23.9 us
  waiting for transfers between devices: 342 us -> 39 us
  Pallas kernels: 0 us -> 227 us
  local copies, waits for them, and re-layouts: 111 us -> 18 us
  other arithmetic: 95.6 us -> 13.7 us
    dot_general x7 -> x4, matrix products: 289 us -> 23.9 us  [the longest x1 8.45 us: local_step(): jnp.einsum('bti,bic->btc', pick, lat_new, preferred_element_type=F32)]
    reduce_scatter x1 -> x0, waiting for transfers between devices: 231 us -> none  [local_step(): reduced = lax.psum_scatter(head_sum, 'tp', scatter_dimension=1, tiled=True)]
    pallas_call x0 -> x1, Pallas kernels: none -> 227 us  [attention_block(): pl.pallas_call(functools.partial(main_kernel, dm), out_shape=jax.ShapeDty...]
    sub x1 -> x0, matrix products: 102 us -> none  [local_step(): attn_probs = jax.nn.softmax(scores, axis=-1).astype(jnp.bfloat16)]
    all_gather x1, waiting for transfers between devices: 110 us -> 39 us  [local_step(): gathered = lax.all_gather(packed, 'tp', axis=1, tiled=True)]
    scatter x25 -> x0, other arithmetic: 67 us -> none
    scatter x48 -> x0, local copies, waits for them, and re-layouts: 53.4 us -> none
    dot_general x1 -> x0, local copies, waits for them, and re-layouts: 50.2 us -> none  [local_step(): jnp.einsum('bsc,chv->bshv', lat_all, w_uv, preferred_element_type=jnp.flo...]
  transfers between devices with their start and end apart: 2 -> 1, of which waited for: 2 -> 1; matrix products, arithmetic and copies ran while one was open for 0% -> 5% of each run, Pallas kernels for 0% -> 0%
where the time goes in v1:
time: 336 us
  Pallas kernels  227 us (68%)
  waiting for transfers between devices  39 us (12%)
  matrix products  23.9 us (7%)
  local copies, waits for them, and re-layouts  18 us (5%)
  between operations  14.2 us (4%)
  other arithmetic  13.7 us (4%)
    pallas_call x1, Pallas kernels, attention_block(): pl.pallas_call(functools.partial(main_kernel, dm), out_shape=jax.ShapeDty...  227 us
    all_gather x1, waiting for transfers between devices, local_step(): gathered = lax.all_gather(packed, 'tp', axis=1, tiled=True)  39 us
    unnamed x34, local copies, waits for them, and re-layouts  8.6 us
    dot_general x1, matrix products, local_step(): jnp.einsum('bti,bic->btc', pick, lat_new, preferred_element_type=F32)  8.45 us
  transfers between devices with their start and end apart: 1, of which 1 were waited for; matrix products, arithmetic and copies ran while one was open for 5% of the time, Pallas kernels for 0%

profile of v1, /device:TPU:112, one launch (start us, length us, event | category | flops | bytes accessed | tf_op | source)
XLA Modules:
  0.0 336.0 jit_solution(5678727185739676073)
XLA Ops:
  7.2 0.0 copy-start.8
  7.2 0.0 copy-start.7
  7.2 0.1 all-gather.2.cloned.1.call-start
  7.3 0.0 copy-start
  7.3 2.6 fusion.4
  9.9 0.0 copy-done.8
  9.9 1.4 copy.29
  11.4 0.0 copy-done.7
  11.4 1.4 copy.30
  12.8 0.0 copy-done
  12.8 0.0 copy-start.13
  12.8 0.0 copy-start.14
  12.8 5.3 %fusion.7 = f32[6,48,576]{2,1,0:T(8,128)S(1)} fusion(bf16[5120,576]{0,1:T(8,128)(2,1)} %param.24, bf16[6,48,5120]{2,1,0:T(8,128)(2,1)S(1)} %copy-done, f32[5120]{0:T(1024)} %param.21, f32[6,48]{1,0:T(8,128)S(1)} %add_rsqrt_fusion.2), kind=kOutput, calls=%fused_computation.10 | convolution fusion | flops 1704591360 | bytes 9532544 | tf_op jit(solution)/shard_map/btd,dk->btk/dot_general | solution.py:419
  18.1 0.0 copy-start.4
  18.1 0.9 copy-done.4
  19.0 0.1 multiply_reduce_fusion.1
  19.1 1.1 copy-done.13
  20.2 0.0 copy-done.14
  20.2 0.0 copy-start.12
  20.2 0.0 copy-start.10
  20.2 6.1 %multiply_reduce_fusion = (f32[6,48]{1,0:T(8,128)S(1)}, f32[6,48,1536]{2,1,0:T(8,128)}) fusion(bf16[5120,1536]{1,0:T(8,128)(2,1)S(1)} %copy-done.13, bf16[6,48,5120]{2,1,0:T(8,128)(2,1)S(1)} %copy-done, f32[5120]{0:T(1024)S(1)} %copy-done.14, f32[6,48]{1,0:T(8,128)S(1)} %add_rsqrt_fusion.2), kind=kOutput, calls=%fused_computation.19 | convolution fusion | flops 4536630784 | bytes 20470016 | tf_op jit(solution)/shard_map/btd,dq->btq/dot_general | solution.py:418
  26.3 0.0 copy-done.12
  26.3 1.2 multiply_convert_fusion.1
  27.5 1.3 add_convert_fusion
  28.8 0.0 copy-done.10
  28.8 1.7 multiply_convert_fusion
  30.5 2.0 concatenate.15
  32.5 0.1 all-gather.2.cloned.1.call-update
  32.6 0.7 neg.3
  33.3 0.0 copy-start.2
  33.3 0.0 copy-start.3
  33.3 1.5 copy.36
  34.8 1.8 slice.25
  36.6 2.2 copy.42
  38.7 2.7 pad_maximum_fusion.2.pe_old_ref
  41.4 0.0 copy-done.2
  41.4 0.0 copy-done.3
  41.4 0.0 copy-start.11
  41.4 0.0 copy-start.5
  41.4 0.0 copy-start.6
  41.4 3.3 pad_maximum_fusion
  44.7 0.0 copy-done.11
  44.7 0.1 compare_and_fusion
  44.8 0.1 iota_subtract_fusion
  44.9 0.0 copy-done.5
  44.9 0.0 copy-done.6
  44.9 4.1 %copy_bitcast_fusion = (bf16[512,2048]{1,0:T(8,128)(2,1)}, bf16[512,2048]{1,0:T(8,128)(2,1)}) fusion(bf16[64,8,16,128]{3,2,1,0:T(8,128)(2,1)S(1)} %bitcast.16, bf16[64,8,16,128]{3,2,1,0:T(8,128)(2,1)S(1)} %bitcast.17), kind=kLoop, calls=%fused_computation.16 | loop fusion | bytes 8388608 | tf_op jit(solution)/shard_map/reshape | solution.py:439
  49.0 39.0 %all-gather.2.cloned.1.call-done.gath_ref = bf16[6,384,2176]{2,1,0:T(8,128)(2,1)} async-done(((bf16[6,48,2176]{2,1,0:T(8,128)(2,1)}), bf16[6,384,2176]{2,1,0:T(8,128)(2,1)}) %all-gather.2.cloned.1.call-update) | async-done | bytes 10027024 | tf_op jit(solution)/shard_map/all_gather | solution.py:425
  88.0 227.1 %attend_project.1 = bf16[6,48,5120]{2,1,0:T(8,128)(2,1)} custom-call(s32[6]{0:T(128)} %len_ref.1, bf16[6,384,2176]{2,1,0:T(8,128)(2,1)} %all-gather.2.cloned.1.call-done.gath_ref, bf16[6,896,512]{2,1,0:T(8,128)(2,1)} %lat_ref.1, bf16[6,512,128]{2,1,0:T(8,128)(2,1)} %pad_maximum_fusion.2.pe_old_ref, f32[6,384,128]{2,1,0:T(8,128)} %get-tuple-element.9.cos_ref, ...), custom_call_target="tpu_custom_call" | custom-call | tf_op jit(solution)/shard_map/attend_project/pallas_call | solution.py:394
  315.0 0.0 copy-start.9
  315.0 8.4 %convert_select_fusion = bf16[6,896,512]{2,1,0:T(8,128)(2,1)} fusion(bf16[6,896,512]{2,1,0:T(8,128)(2,1)} %lat_ref.1, pred[6,896]{1,0:T(8,128)(4,1)S(1)} %compare_and_fusion, s32[6,896]{1,0:T(8,128)S(1)} %iota_subtract_fusion, bf16[6,384,2176]{2,1,0:T(8,128)(2,1)} %all-gather.2.cloned.1.call-done.gath_ref), kind=kOutput, calls=%fused_computation.12 | convolution fusion | flops 2121498624 | bytes 13396224 | tf_op jit(solution)/shard_map/bti,bic->btc/dot_general | solution.py:431
  323.5 0.0 copy-done.9
  323.5 0.0 copy-start.1
  323.5 4.0 %fusion.15 = bf16[6,896,64]{1,2,0:T(8,128)(2,1)} fusion(bf16[6,896,64]{1,2,0:T(8,128)(2,1)S(1)} %copy-done.9, s32[6,896]{1,0:T(8,128)S(1)} %iota_subtract_fusion, pred[6,896]{1,0:T(8,128)(4,1)S(1)} %compare_and_fusion, bf16[6,384,2176]{2,1,0:T(8,128)(2,1)} %all-gather.2.cloned.1.call-done.gath_ref), kind=kOutput, calls=%fused_computation.23 | convolution fusion | flops 266993664 | bytes 1992960 | tf_op jit(solution)/shard_map/bti,bic->btc/dot_general | solution.py:432
  327.5 0.0 copy-done.1
  327.5 1.6 copy.48
  (3 shorter events, 0.0 us)
Async XLA Ops:
  7.2 2.8 copy-start.8
  7.2 4.2 %copy-start.7 = (f32[6,384,32]{1,2,0:T(8,128)S(1)}, f32[6,384,32]{1,2,0:T(8,128)}, u32[]{:S(2)}) copy-start(f32[6,384,32]{1,2,0:T(8,128)} %param.18) | copy-start | bytes 884740
  7.2 80.8 %all-gather.2.cloned.1.call-start = ((), (), s32[]{:S(2)}) async-start(), calls=%async_computation | async-start | bytes 11280384 | tf_op jit(solution)/shard_map/all_gather | solution.py:425
  7.3 5.5 %copy-start = (bf16[6,48,5120]{2,1,0:T(8,128)(2,1)S(1)}, bf16[6,48,5120]{2,1,0:T(8,128)(2,1)}, u32[]{:S(2)}) copy-start(bf16[6,48,5120]{2,1,0:T(8,128)(2,1)} %hid_ref.1) | copy-start | bytes 8847364
  12.8 7.5 %copy-start.13 = (bf16[5120,1536]{1,0:T(8,128)(2,1)S(1)}, bf16[5120,1536]{1,0:T(8,128)(2,1)}, u32[]{:S(2)}) copy-start(bf16[5120,1536]{1,0:T(8,128)(2,1)} %param.22) | copy-start | bytes 47185924
  12.8 7.5 %copy-start.14 = (f32[5120]{0:T(1024)S(1)}, f32[5120]{0:T(1024)}, u32[]{:S(2)}) copy-start(f32[5120]{0:T(1024)} %param.21) | copy-start | bytes 61444
  18.1 0.9 copy-start.4
  20.2 6.1 %copy-start.12 = (f32[512]{0:T(512)S(1)}, f32[512]{0:T(512)}, u32[]{:S(2)}) copy-start(f32[512]{0:T(512)} %param.25) | copy-start | bytes 6148
  20.2 8.5 %copy-start.10 = (f32[1536]{0:T(1024)S(1)}, f32[1536]{0:T(1024)}, u32[]{:S(2)}) copy-start(f32[1536]{0:T(1024)} %param.23) | copy-start | bytes 18436
  33.3 8.1 %copy-start.2 = (f32[6,384,32]{2,1,0:T(8,128)S(1)}, f32[6,384,32]{2,1,0:T(8,128)}, u32[]{:S(2)}) copy-start(f32[6,384,32]{2,1,0:T(8,128)} %copy.29) | copy-start | bytes 884740
  33.3 8.1 %copy-start.3 = (f32[6,384,32]{2,1,0:T(8,128)S(1)}, f32[6,384,32]{2,1,0:T(8,128)}, u32[]{:S(2)}) copy-start(f32[6,384,32]{2,1,0:T(8,128)} %copy.30) | copy-start | bytes 884740
  41.4 3.3 copy-start.11
  41.4 3.5 %copy-start.5 = (bf16[512,16,128]{2,1,0:T(8,128)(2,1)S(1)}, bf16[512,16,128]{2,1,0:T(8,128)(2,1)}, u32[]{:S(2)}) copy-start(bf16[512,16,128]{2,1,0:T(8,128)(2,1)} %param.28) | copy-start | bytes 6291460
  41.4 3.4 %copy-start.6 = (bf16[512,16,128]{2,1,0:T(8,128)(2,1)S(1)}, bf16[512,16,128]{2,1,0:T(8,128)(2,1)}, u32[]{:S(2)}) copy-start(bf16[512,16,128]{2,1,0:T(8,128)(2,1)} %param.27) | copy-start | bytes 6291460
  315.0 8.5 %copy-start.9 = (bf16[6,896,64]{1,2,0:T(8,128)(2,1)S(1)}, bf16[6,896,64]{1,2,0:T(8,128)(2,1)}, u32[]{:S(2)}) copy-start(bf16[6,896,64]{1,2,0:T(8,128)(2,1)} %param.20) | copy-start | bytes 2064388
  323.5 4.0 %copy-start.1 = (bf16[6,48,5120]{2,1,0:T(8,128)(2,1)S(1)}, bf16[6,48,5120]{2,1,0:T(8,128)(2,1)}, u32[]{:S(2)}) copy-start(bf16[6,48,5120]{2,1,0:T(8,128)(2,1)} %attend_project.1) | copy-start | bytes 8847364
Sparse Core Ops, SparseCore 0:
  32.7 55.2 all-gather.1

commit v2 on v0

v2 whole, which is shorter than its diff:
```python
import functools
import types

import jax
import jax.numpy as jnp
from jax import lax
from jax.experimental import pallas as pl
from jax.experimental.pallas import tpu as pltpu
from jax.sharding import PartitionSpec as P

BF16 = jnp.bfloat16
F32 = jnp.float32
NEG = -1e30
LOG2E = 1.4426950408889634
EPS = 1e-6
QBLK = 128
CORES = 2
MAIN_ID = 0
PANEL = 256
RELAY_ROWS = 64
RELAY_SLOTS = 4


def rms_norm(values, gain_vec):
    mean_sq = jnp.sum(values * values, axis=-1, keepdims=True) * (1.0 / values.shape[-1])
    return values * lax.rsqrt(mean_sq + EPS) * gain_vec


def dot_nn(lhs, rhs):
    return lax.dot_general(lhs, rhs, (((1,), (0,)), ((), ())), preferred_element_type=F32)


def dot_nt(lhs, rhs):
    return lax.dot_general(lhs, rhs, (((1,), (1,)), ((), ())), preferred_element_type=F32)


def rope_pair(values, cos_tab, sin_tab, half_dim):
    lanes = values.shape[1]
    upper = pltpu.roll(values, lanes - half_dim, 1)
    lower = pltpu.roll(values, half_dim, 1)
    lane = lax.broadcasted_iota(jnp.int32, values.shape, 1)
    swapped = jnp.where(lane % (2 * half_dim) < half_dim, upper, lower)
    return values * cos_tab + swapped * sin_tab


KIND_PARTNER, KIND_LEFT, KIND_RIGHT, KIND_LEFT_PARTNER, KIND_RIGHT_PARTNER, KIND_LEFT_RIGHT, KIND_RIGHT_LEFT, KIND_FAR_A, KIND_FAR_B = range(9)
KINDS = 9
INPUTS = ("length", "hid", "cos", "sin", "lat", "pe", "g_in", "w_dq", "g_q", "w_dkv", "g_kv", "wuq", "wuk", "wuv", "wout")
OUTPUTS = ("out", "gath_q", "gath_kv")


def main_kernel(dm, names, *refs):
    r = types.SimpleNamespace(**dict(zip(names, refs, strict=True)))
    me = lax.axis_index("tp")
    chip = me // CORES
    core = me % CORES
    chips = dm.chips
    left_chip = (chip + chips - 1) % chips
    right_chip = (chip + 1) % chips
    far_chip = (chip + 2) % chips
    partner = chip * CORES + (1 - core)
    left = left_chip * CORES + core
    right = right_chip * CORES + core

    groups, gh = dm.groups, dm.group_heads
    chunks, cw, hw, tok = dm.chunks, dm.chunk_cols, dm.half_cols, dm.tok
    seqs = dm.seqs
    attn_ticks = seqs * groups
    out_ticks = seqs * chunks
    nope, rope, vdim, prefix, qlen = dm.nope, dm.rope, dm.vdim, dm.prefix, dm.qlen
    nslot = dm.ring_slots
    q_rank, kv_rank, model = dm.q_rank, dm.kv_rank, dm.model
    kv_cols = kv_rank + 2 * rope
    rows_own = seqs * tok

    def hidden_copy(b):
        return pltpu.make_async_copy(r.hid.at[b], r.act.at[pl.ds(b * tok, tok)], r.act_sem.at[b])

    def small_copies():
        return (
            pltpu.make_async_copy(r.g_in, r.gain_in.at[0], r.small_sem.at[0]),
            pltpu.make_async_copy(r.g_q, r.gain_q.at[0], r.small_sem.at[1]),
            pltpu.make_async_copy(r.g_kv, r.gain_kv.at[0], r.small_sem.at[2]),
            pltpu.make_async_copy(r.cos, r.cos_raw, r.small_sem.at[3]),
            pltpu.make_async_copy(r.sin, r.sin_raw, r.small_sem.at[4]),
        )

    def w_dkv_copies():
        return (
            pltpu.make_async_copy(r.w_dkv, r.wkv_down.at[pl.ds(0, kv_rank + rope)], r.wkv_sem.at[0]),
            pltpu.make_async_copy(r.w_dkv.at[pl.ds(kv_rank, rope)], r.wkv_down.at[pl.ds(kv_rank + rope, rope)], r.wkv_sem.at[1]),
        )

    def w_dq_copies(s):
        return tuple(
            pltpu.make_async_copy(r.w_dq.at[:, pl.ds((2 * s + p) * PANEL, PANEL)], r.wbuf.at[s % 2, pl.ds(p * model, model)], r.wbuf_sem.at[s % 2, p])
            for p in range(2)
        )

    def wout_copies(j):
        depth = r.wout.shape[0]
        return tuple(
            pltpu.make_async_copy(r.wout.at[:, pl.ds((j % chunks) * cw + p * PANEL, PANEL)], r.wbuf.at[j % 2, pl.ds(p * depth, depth)], r.wbuf_sem.at[j % 2, p])
            for p in range(cw // PANEL)
        )

    def relay_copy(src, n):
        slot = n % RELAY_SLOTS
        block = n % (kv_rank // RELAY_ROWS)
        return pltpu.make_async_copy(src.at[pl.ds(block * RELAY_ROWS, RELAY_ROWS)], r.relay.at[slot].reshape(RELAY_ROWS, dm.heads, nope), r.relay_sem.at[slot])

    def seq_copies(b):
        slot = b % 2
        return (
            pltpu.make_async_copy(r.gath_q.at[b], r.q_lat.at[slot], r.seq_sem.at[slot, 0]),
            pltpu.make_async_copy(r.lat.at[b, pl.ds(0, prefix)], r.lat_buf.at[slot, pl.ds(0, prefix)], r.seq_sem.at[slot, 1]),
            pltpu.make_async_copy(r.gath_kv.at[b, :, pl.ds(0, kv_rank)], r.lat_buf.at[slot, pl.ds(prefix, qlen)], r.seq_sem.at[slot, 2]),
            pltpu.make_async_copy(r.pe.at[b, :, pl.ds(0, prefix)], r.pe_old.at[slot], r.seq_sem.at[slot, 3]),
            pltpu.make_async_copy(r.gath_kv.at[b, :, pl.ds(kv_rank, 2 * rope)], r.pe_new.at[slot], r.seq_sem.at[slot, 4]),
        )

    def wuq_copies(i):
        g, slot = i % groups, i % 2
        return (
            pltpu.make_async_copy(r.wuq.at[pl.ds(g * gh, gh), pl.ds(0, nope)], r.wuq_buf.at[slot, pl.ds(0, gh * nope)].reshape(gh, nope, q_rank), r.wuq_sem.at[slot, 0]),
            pltpu.make_async_copy(r.wuq.at[pl.ds(g * gh, gh), pl.ds(nope, rope)], r.wuq_buf.at[slot, pl.ds(gh * nope, gh * rope)].reshape(gh, rope, q_rank), r.wuq_sem.at[slot, 1]),
        )

    def hid_copy(j):
        return pltpu.make_async_copy(r.hid.at[j // chunks, :, pl.ds((j % chunks) * cw, cw)], r.hid_buf.at[j % nslot], r.hid_sem.at[j % nslot])

    def y_copy(j):
        return pltpu.make_async_copy(r.y_buf.at[j % 2], r.out.at[j // chunks, :, pl.ds((j % chunks) * cw, cw)], r.y_sem.at[j % 2])

    half = tok // 2

    def gather_unit(b, is_q):
        dst = r.gath_q if is_q else r.gath_kv
        src = r.pack_q if is_q else r.pack_kv
        unit = b + (seqs if is_q else 0)

        def copy(kind, source, owner, offset, count, peer):
            rows = pl.ds(pl.multiple_of(owner * tok + offset, 8), count)
            return pltpu.make_async_remote_copy(
                src_ref=source if source is not None else dst.at[b, rows],
                dst_ref=dst.at[b, rows],
                send_sem=r.gath_send.at[unit, kind],
                recv_sem=r.gath_recv.at[unit, kind],
                device_id={"tp": peer},
            )

        far = far_chip * CORES + core
        return {
            KIND_PARTNER: lambda: copy(KIND_PARTNER, src.at[b], me, 0, tok, partner),
            KIND_LEFT: lambda: copy(KIND_LEFT, src.at[b], me, 0, tok, left),
            KIND_RIGHT: lambda: copy(KIND_RIGHT, src.at[b], me, 0, tok, right),
            KIND_LEFT_PARTNER: lambda: copy(KIND_LEFT_PARTNER, None, left, 0, tok, partner),
            KIND_RIGHT_PARTNER: lambda: copy(KIND_RIGHT_PARTNER, None, right, 0, tok, partner),
            KIND_LEFT_RIGHT: lambda: copy(KIND_LEFT_RIGHT, None, left, 0, half, right),
            KIND_RIGHT_LEFT: lambda: copy(KIND_RIGHT_LEFT, None, right, half, half, left),
            KIND_FAR_A: lambda: copy(KIND_FAR_A, None, far, 0, half, partner),
            KIND_FAR_B: lambda: copy(KIND_FAR_B, None, far, half, half, partner),
        }

    def local_copy(b, is_q):
        dst = r.gath_q if is_q else r.gath_kv
        src = r.pack_q if is_q else r.pack_kv
        unit = b + (seqs if is_q else 0)
        return pltpu.make_async_copy(src.at[b], dst.at[b, pl.ds(pl.multiple_of(me * tok, 8), tok)], r.local_sem.at[unit])

    scope = jax.named_scope

    def gather_send(b, is_q):
        copies = gather_unit(b, is_q)
        copies[KIND_LEFT]().start()
        copies[KIND_RIGHT]().start()
        copies[KIND_PARTNER]().start()
        local_copy(b, is_q).start()

    def gather_forward(b, is_q):
        copies = gather_unit(b, is_q)
        copies[KIND_RIGHT]().wait_recv()
        copies[KIND_LEFT_RIGHT]().start()
        copies[KIND_LEFT_PARTNER]().start()
        copies[KIND_LEFT]().wait_recv()
        copies[KIND_RIGHT_LEFT]().start()
        copies[KIND_RIGHT_PARTNER]().start()

    def gather_far(b, is_q):
        copies = gather_unit(b, is_q)
        copies[KIND_LEFT_RIGHT]().wait_recv()
        copies[KIND_FAR_A]().start()
        copies[KIND_RIGHT_LEFT]().wait_recv()
        copies[KIND_FAR_B]().start()

    def gather_done(b, is_q):
        copies = gather_unit(b, is_q)
        for kind in (KIND_PARTNER, KIND_LEFT_PARTNER, KIND_RIGHT_PARTNER, KIND_FAR_A, KIND_FAR_B):
            copies[kind]().wait_recv()
        local_copy(b, is_q).wait()

    def gather_drain(b, is_q):
        copies = gather_unit(b, is_q)
        for kind in range(KINDS):
            copies[kind]().wait_send()

    def xch_copy(j, t):
        slot = j % 2
        return pltpu.make_async_remote_copy(
            src_ref=r.part.at[pl.ds(pl.multiple_of((t * CORES + 1 - core) * tok, 8), tok), pl.ds(0, cw)],
            dst_ref=r.xch.at[slot, t],
            send_sem=r.xch_send.at[slot, t],
            recv_sem=r.xch_recv.at[slot, t],
            device_id={"tp": partner},
        )

    def toward(u):
        if u == 0:
            return left, left_chip, right, right_chip
        return right, right_chip, left, left_chip

    def ring_copy(name, j, u, block, peer):
        slot = j % nslot
        return pltpu.make_async_remote_copy(
            src_ref=r.sums.at[slot, block, :, pl.ds(u * hw, hw)],
            dst_ref=getattr(r, name).at[slot, u],
            send_sem=getattr(r, name + "_send").at[slot, u],
            recv_sem=getattr(r, name + "_recv").at[slot, u],
            device_id={"tp": peer},
        )

    def hop_copy(j, u):
        down, _, _, _ = toward(u)
        return ring_copy("hop", j, u, far_chip, down)

    def direct_copy(j, u):
        _, _, up, up_chip = toward(u)
        return ring_copy("direct", j, u, up_chip, up)

    def final_copy(j, u):
        down, down_chip, _, _ = toward(u)
        return ring_copy("final", j, u, down_chip, down)

    def attention(b, g, wslot):
        slot = b % 2
        q_lat = r.q_lat[slot]
        lane = lax.broadcasted_iota(jnp.int32, (qlen, 2 * rope), 1)
        q_pe = dot_nt(q_lat, r.wuq_buf[wslot, gh * nope:])
        for pair in range(gh // 2):
            rotated = rope_pair(q_pe[:, pair * 2 * rope:(pair + 1) * 2 * rope], r.cos_tab[b], r.sin_tab[b], rope // 2)
            r.qcat[2 * pair, :, nope:] = jnp.where(lane < rope, rotated, 0.0).astype(BF16)
            r.qcat[2 * pair + 1, :, nope:] = jnp.where(lane >= rope, rotated, 0.0).astype(BF16)
        q_nope = dot_nt(q_lat, r.wuq_buf[wslot, :gh * nope])
        for h in range(gh):
            r.qcat[h, :, :nope] = q_nope[:, h * nope:(h + 1) * nope].astype(BF16)
        keys = dot_nn(r.lat_buf[slot], r.wkv_up[0, g])
        for h in range(gh):
            r.kcat[h, :, :nope] = keys[:, h * nope:(h + 1) * nope].astype(BF16)
        r.vcat[...] = dot_nn(r.lat_buf[slot], r.wkv_up[1, g]).astype(BF16)

        key_pos = lax.broadcasted_iota(jnp.int32, (1, prefix), 1)
        bias = jnp.where(key_pos < r.length[b], 0.0, NEG).astype(F32)
        row = lax.broadcasted_iota(jnp.int32, (QBLK, QBLK), 0)
        col = lax.broadcasted_iota(jnp.int32, (QBLK, QBLK), 1)
        causal = col <= row
        nblk = qlen // QBLK
        wide = prefix + (nblk - 1) * QBLK
        for h in range(gh):
            main = dot_nt(r.qcat[h], r.kcat[h, :wide])
            last = dot_nt(r.qcat[h, (nblk - 1) * QBLK:], r.kcat[h, wide:])
            for blk in range(nblk):
                rows = slice(blk * QBLK, (blk + 1) * QBLK)
                pieces = [main[rows, :prefix] + bias]
                if blk == nblk - 1:
                    pieces.append(main[rows, prefix:wide])
                    diag = last
                else:
                    if blk > 0:
                        pieces.append(main[rows, prefix:prefix + blk * QBLK])
                    diag = main[rows, prefix + blk * QBLK:prefix + (blk + 1) * QBLK]
                pieces.append(jnp.where(causal, diag, NEG))
                top = functools.reduce(jnp.maximum, [jnp.max(piece, axis=1, keepdims=True) for piece in pieces])
                total = None
                acc = None
                start = 0
                for piece in pieces:
                    prob = jnp.exp2((piece - top) * dm.exp_scale)
                    piece_sum = jnp.sum(prob, axis=1, keepdims=True)
                    width = piece.shape[1]
                    term = dot_nn(prob.astype(BF16), r.vcat[start:start + width, h * vdim:(h + 1) * vdim])
                    total = piece_sum if total is None else total + piece_sum
                    acc = term if acc is None else acc + term
                    start += width
                r.attn[slot, rows, pl.ds(pl.multiple_of((g * gh + h) * vdim, 128), vdim)] = (acc / total).astype(BF16)

    for copy in small_copies():
        copy.start()
    for b in range(seqs):
        hidden_copy(b).start()
    for copy in w_dkv_copies():
        copy.start()

    barrier = pltpu.get_barrier_semaphore()
    for peer in (partner, left, right):
        pl.semaphore_signal(barrier, inc=1, device_id={"tp": peer})

    with scope("w_small"):
        for copy in small_copies():
            copy.wait()

    def rope_table(b, carry):
        cos_rows, sin_rows = r.cos_raw[b], r.sin_raw[b]
        r.cos_tab[b] = jnp.concatenate([cos_rows] * 4, axis=0).T
        r.sin_tab[b] = jnp.concatenate([-sin_rows, sin_rows] * 2, axis=0).T
        return carry

    for copy in w_dq_copies(0) + w_dq_copies(1):
        copy.start()

    with scope("rope_tab"):
        lax.fori_loop(0, seqs, rope_table, 0)

    norm_rows = 16

    def norm_step(n, carry):
        hidden_copy(n).wait()
        for part in range(tok // norm_rows):
            rows = pl.ds(pl.multiple_of(n * tok + part * norm_rows, norm_rows), norm_rows)
            r.act[rows] = rms_norm(r.act[rows].astype(F32), r.gain_in[...]).astype(BF16)
        return carry

    with scope("norm"):
        lax.fori_loop(0, seqs, norm_step, 0)

    with scope("w_dkv"):
        for copy in w_dkv_copies():
            copy.wait()
    with scope("dkv"):
        r.part[:rows_own, :kv_cols] = dot_nt(r.act[...], r.wkv_down[...])

    blocks = kv_rank // RELAY_ROWS
    for n in range(RELAY_SLOTS):
        relay_copy(r.wuk, n).start()
    for copy in wuq_copies(0):
        copy.start()

    with scope("w_barrier"):
        pl.semaphore_wait(barrier, 3)

    def kv_step(b, carry):
        rows = pl.ds(pl.multiple_of(b * tok, 16), tok)
        own = pl.ds(pl.multiple_of(me * tok, 16), tok)
        r.pack_kv[b, :, :kv_rank] = rms_norm(r.part[rows, :kv_rank], r.gain_kv[...]).astype(BF16)
        r.pack_kv[b, :, kv_rank:] = rope_pair(r.part[rows, kv_rank:kv_cols], r.cos_tab[b, own], r.sin_tab[b, own], rope // 2).astype(BF16)
        return carry

    lax.fori_loop(0, seqs, kv_step, 0)

    def kv_send(b, carry):
        gather_send(b, False)
        return carry

    with scope("kv_send"):
        lax.fori_loop(0, seqs, kv_send, 0)

    def dq_step(s, carry):
        for copy in w_dq_copies(s):
            copy.wait()
        act = r.act[...]
        for p in range(2):
            cols = pl.ds(pl.multiple_of((2 * s + p) * PANEL, PANEL), PANEL)
            r.part[:rows_own, cols] = dot_nn(act, r.wbuf[s % 2, p * model:(p + 1) * model])

        @pl.when(s + 2 < q_rank // (2 * PANEL))
        def _():
            for copy in w_dq_copies(s + 2):
                copy.start()

        return carry

    with scope("dq"):
        lax.fori_loop(0, q_rank // (2 * PANEL), dq_step, 0)

    def q_step(b, carry):
        rows = pl.ds(pl.multiple_of(b * tok, 16), tok)
        r.pack_q[b] = rms_norm(r.part[rows, :q_rank], r.gain_q[...]).astype(BF16)
        return carry

    lax.fori_loop(0, seqs, q_step, 0)

    with scope("send_q0"):
        gather_send(0, True)
        gather_forward(0, False)
        gather_send(1, True)

    def relay_step(n, carry):
        slot = n % RELAY_SLOTS
        relay_copy(r.wuk, n).wait()
        r.relay_f32[...] = r.relay[slot].astype(F32)

        @pl.when(n + RELAY_SLOTS < blocks)
        def _():
            relay_copy(r.wuk, n + RELAY_SLOTS).start()

        @pl.when(jnp.logical_and(n + RELAY_SLOTS >= blocks, n + RELAY_SLOTS < 2 * blocks))
        def _():
            relay_copy(r.wuv, n + RELAY_SLOTS).start()

        rows = pl.ds(pl.multiple_of((n % blocks) * RELAY_ROWS, RELAY_ROWS), RELAY_ROWS)
        for h in range(dm.heads):
            head_rows = r.relay_f32[pl.ds(h, RELAY_ROWS, stride=dm.heads), :]
            r.wkv_up[n // blocks, h // gh, rows, (h % gh) * nope:(h % gh + 1) * nope] = head_rows.astype(BF16)
        return carry

    with scope("relay"):
        lax.fori_loop(0, 2 * blocks, relay_step, 0)

    with scope("fwd_q0"):
        gather_forward(0, True)

    def kv_forward(b, carry):
        gather_forward(b, False)
        return carry

    with scope("kv_fwd"):
        gather_send(2, True)
        gather_send(3, True)
        lax.fori_loop(1, seqs, kv_forward, 0)
    with scope("far0"):
        gather_far(0, False)
        gather_far(0, True)
    with scope("done0"):
        gather_done(0, False)
        gather_done(0, True)
    for copy in seq_copies(0):
        copy.start()

    gather_plan = (
        (0, [(gather_forward, 1, True), (gather_send, 4, True)]),
        (1, [(gather_forward, 2, True), (gather_forward, 3, True), (gather_send, 5, True)]),
        (2, [(gather_far, 1, True)] + [(gather_far, v, False) for v in range(1, seqs)]),
        (3, [(gather_forward, 4, True)]),
        (4, [(gather_forward, 5, True), (gather_far, 2, True), (gather_far, 3, True)]),
        (5, [(gather_far, 4, True)]),
        (6, [(gather_far, 5, True)]),
    )

    def tick(i, carry):
        b = i // groups
        g = i % groups
        wslot = i % 2

        for at, steps in gather_plan:
            @pl.when(i == at)
            def _():
                with scope("t_gather"):
                    for step, seq, is_q in steps:
                        if seq < seqs:
                            step(seq, is_q)

        @pl.when(i + 1 < attn_ticks)
        def _():
            for copy in wuq_copies(i + 1):
                copy.start()

        @pl.when(jnp.logical_and(g == groups - 1, b + 1 < seqs))
        def _():
            with scope("t_done"):
                gather_done(b + 1, False)
                gather_done(b + 1, True)
            for copy in seq_copies(b + 1):
                copy.start()

        j_next = i + 1 - groups

        @pl.when(jnp.logical_and(j_next >= 0, j_next < out_ticks))
        def _():
            for copy in wout_copies(j_next):
                copy.start()

        j1 = i - groups - 1

        @pl.when(jnp.logical_and(j1 >= 0, j1 < out_ticks))
        def _():
            hid_copy(j1).start()
            with scope("w_xch"):
                for t in range(chips):
                    xch_copy(j1, t).wait_recv()
            for off in (2, 1, 3, 0):
                t = (chip + off) % chips
                rows = pl.ds(pl.multiple_of((t * CORES + core) * tok, 8), tok)
                r.sums[j1 % nslot, t] = r.part[rows, :cw] + r.xch[j1 % 2, t]

            @pl.when(j1 + 2 < out_ticks)
            def _():
                pl.semaphore_signal(r.credit_pair, inc=1, device_id={"tp": partner})

            @pl.when(j1 >= nslot)
            def _():
                with scope("w_credit"):
                    pl.semaphore_wait(r.credit_left, 1)
                    pl.semaphore_wait(r.credit_right, 1)

            for u in range(2):
                hop_copy(j1, u).start()
            for u in range(2):
                direct_copy(j1, u).start()

        j2 = i - groups - 2

        @pl.when(jnp.logical_and(j2 >= 0, j2 < out_ticks))
        def _():
            with scope("w_hop"):
                for u in range(2):
                    hop_copy(j2, u).wait_recv()
            for u in range(2):
                _, down_chip, _, _ = toward(u)
                cols = pl.ds(u * hw, hw)
                r.sums[j2 % nslot, down_chip, :, cols] = r.sums[j2 % nslot, down_chip, :, cols] + r.hop[j2 % nslot, u]
            for u in range(2):
                final_copy(j2, u).start()

        j3 = i - groups - 4

        @pl.when(jnp.logical_and(j3 >= 0, j3 < out_ticks))
        def _():
            s3 = j3 % nslot
            hid_copy(j3).wait()

            @pl.when(j3 >= 2)
            def _():
                y_copy(j3 - 2).wait()

            with scope("w_final"):
                for u in range(2):
                    direct_copy(j3, u).wait()
                    final_copy(j3, u).wait()
                    hop_copy(j3, u).wait_send()
            for u in range(2):
                cols = pl.ds(u * hw, hw)
                total = r.sums[s3, chip, :, cols] + r.direct[s3, u] + r.final[s3, u]
                r.y_buf[j3 % 2, :, cols] = (total + r.hid_buf[s3, :, cols].astype(F32)).astype(BF16)

            @pl.when(j3 + nslot < out_ticks)
            def _():
                pl.semaphore_signal(r.credit_left, inc=1, device_id={"tp": right})
                pl.semaphore_signal(r.credit_right, inc=1, device_id={"tp": left})

            y_copy(j3).start()

        j0 = i - groups

        @pl.when(jnp.logical_and(j0 >= 0, j0 < out_ticks))
        def _():
            @pl.when(j0 >= 1)
            def _():
                for t in range(chips):
                    xch_copy(j0 - 1, t).wait_send()

            with scope("w_wout"):
                for copy in wout_copies(j0):
                    copy.wait()
            with scope("project"):
                attn = r.attn[(j0 // chunks) % 2]
                depth = attn.shape[1]
                for p in range(cw // PANEL):
                    r.part[:, p * PANEL:(p + 1) * PANEL] = dot_nn(attn, r.wbuf[j0 % 2, p * depth:(p + 1) * depth])

            @pl.when(j0 >= 2)
            def _():
                pl.semaphore_wait(r.credit_pair, 1)

            for t in range(chips):
                xch_copy(j0, t).start()

        @pl.when(i < attn_ticks)
        def _():
            @pl.when(g == 0)
            def _():
                with scope("w_seq"):
                    for copy in seq_copies(b):
                        copy.wait()
                old_rows = r.pe_old[b % 2].astype(F32)
                old_pe = jnp.concatenate([old_rows, old_rows], axis=0).T.astype(BF16)
                for h in range(gh):
                    r.kcat[h, :prefix, nope:] = old_pe
                    r.kcat[h, prefix:, nope:] = r.pe_new[b % 2]

            with scope("w_wuq"):
                for copy in wuq_copies(i):
                    copy.wait()
            with scope("attend"):
                attention(b, g, wslot)

        return carry

    lax.fori_loop(0, out_ticks + groups + 4, tick, 0)

    for t in range(chips):
        xch_copy(out_ticks - 1, t).wait_send()
    for j in (out_ticks - 2, out_ticks - 1):
        y_copy(j).wait()

    def drain(b, carry):
        gather_drain(b, False)
        gather_drain(b, True)
        return carry

    lax.fori_loop(0, seqs, drain, 0)


def attention_block(tp, length, hid, cos, sin, lat, pe, g_in, w_dq, g_q, w_dkv, g_kv, wuq, wuk, wuv, wout):
    dm = types.SimpleNamespace()
    dm.seqs, dm.tok, dm.model = hid.shape
    dm.heads, head_dim, dm.q_rank = wuq.shape
    dm.kv_rank, _, dm.nope = wuk.shape
    dm.vdim = wuv.shape[2]
    dm.rope = head_dim - dm.nope
    dm.qlen = dm.tok * tp
    dm.prefix = lat.shape[1] - dm.qlen
    dm.chips = tp // CORES
    dm.group_heads = 4
    dm.groups = dm.heads // dm.group_heads
    dm.chunks = 4
    dm.chunk_cols = dm.model // dm.chunks
    dm.half_cols = dm.chunk_cols // 2
    dm.ring_slots = 4
    dm.exp_scale = head_dim ** -0.5 * LOG2E
    gh, keys, ns, kv_cols = dm.group_heads, dm.prefix + dm.qlen, dm.ring_slots, dm.kv_rank + 2 * dm.rope
    assert dm.chips == 4 and dm.groups == dm.chunks and dm.vdim == dm.nope

    def vmem(*shape, dtype=BF16):
        return pltpu.VMEM(shape, dtype)

    def dma(*shape):
        return pltpu.SemaphoreType.DMA(shape)

    wbuf_rows = max(2 * dm.model, (dm.chunk_cols // PANEL) * dm.heads * dm.vdim)
    part_cols = max(dm.chunk_cols, dm.q_rank)
    ring = (ns, 2, dm.tok, dm.half_cols)
    credit = pltpu.SemaphoreType.REGULAR
    scratch = dict(
        act=vmem(dm.seqs * dm.tok, dm.model),
        gain_in=vmem(1, dm.model, dtype=F32), gain_q=vmem(1, dm.q_rank, dtype=F32), gain_kv=vmem(1, dm.kv_rank, dtype=F32),
        cos_raw=vmem(*cos.shape, dtype=F32), sin_raw=vmem(*cos.shape, dtype=F32),
        cos_tab=vmem(dm.seqs, dm.qlen, 2 * dm.rope, dtype=F32), sin_tab=vmem(dm.seqs, dm.qlen, 2 * dm.rope, dtype=F32),
        wkv_down=vmem(kv_cols, dm.model),
        wbuf=vmem(2, wbuf_rows, PANEL),
        part=vmem(dm.qlen, part_cols, dtype=F32),
        pack_q=vmem(dm.seqs, dm.tok, dm.q_rank), pack_kv=vmem(dm.seqs, dm.tok, kv_cols),
        relay=vmem(RELAY_SLOTS, RELAY_ROWS * dm.heads, dm.nope), relay_f32=vmem(RELAY_ROWS * dm.heads, dm.nope, dtype=F32),
        wkv_up=vmem(2, dm.groups, dm.kv_rank, gh * dm.nope),
        q_lat=vmem(2, dm.qlen, dm.q_rank),
        lat_buf=vmem(2, keys, dm.kv_rank),
        pe_old=vmem(2, dm.rope, dm.prefix), pe_new=vmem(2, dm.qlen, 2 * dm.rope),
        wuq_buf=vmem(2, gh * head_dim, dm.q_rank),
        qcat=vmem(gh, dm.qlen, dm.nope + 2 * dm.rope), kcat=vmem(gh, keys, dm.nope + 2 * dm.rope), vcat=vmem(keys, gh * dm.vdim),
        attn=vmem(2, dm.qlen, dm.heads * dm.vdim),
        xch=vmem(2, dm.chips, dm.tok, dm.chunk_cols, dtype=F32),
        sums=vmem(ns, dm.chips, dm.tok, dm.chunk_cols, dtype=F32),
        hop=vmem(*ring, dtype=F32), direct=vmem(*ring, dtype=F32), final=vmem(*ring, dtype=F32),
        hid_buf=vmem(ns, dm.tok, dm.chunk_cols), y_buf=vmem(2, dm.tok, dm.chunk_cols),
        act_sem=dma(dm.seqs), small_sem=dma(5), wkv_sem=dma(2), wbuf_sem=dma(2, max(2, dm.chunk_cols // PANEL)), relay_sem=dma(RELAY_SLOTS),
        seq_sem=dma(2, 5), wuq_sem=dma(2, 2), hid_sem=dma(ns), y_sem=dma(2),
        local_sem=dma(2 * dm.seqs), gath_send=dma(2 * dm.seqs, KINDS), gath_recv=dma(2 * dm.seqs, KINDS),
        xch_send=dma(2, dm.chips), xch_recv=dma(2, dm.chips),
        hop_send=dma(ns, 2), hop_recv=dma(ns, 2), direct_send=dma(ns, 2), direct_recv=dma(ns, 2), final_send=dma(ns, 2), final_recv=dma(ns, 2),
        credit_pair=credit, credit_left=credit, credit_right=credit,
    )
    hbm = pl.BlockSpec(memory_space=pl.ANY)
    block_out, _, gath_kv = pl.pallas_call(
        functools.partial(main_kernel, dm, INPUTS + OUTPUTS + tuple(scratch)),
        out_shape=(
            jax.ShapeDtypeStruct(hid.shape, BF16),
            jax.ShapeDtypeStruct((dm.seqs, dm.qlen, dm.q_rank), BF16),
            jax.ShapeDtypeStruct((dm.seqs, dm.qlen, kv_cols), BF16),
        ),
        in_specs=[pl.BlockSpec(memory_space=pltpu.SMEM)] + [hbm] * (len(INPUTS) - 1),
        out_specs=(hbm, hbm, hbm),
        scratch_shapes=list(scratch.values()),
        compiler_params=pltpu.CompilerParams(collective_id=MAIN_ID, has_side_effects=True, vmem_limit_bytes=67_000_000),
        name="attend_project",
    )(length, hid, cos, sin, lat, pe, g_in, w_dq, g_q, w_dkv, g_kv, wuq, wuk, wuv, wout)
    return block_out, gath_kv


def cache_kernel(kv_rank, len_ref, lat_ref, pe_ref, new_ref, y_ref, lat_out, pe_out, y_out):
    length = len_ref[pl.program_id(0)]
    rows, count = lat_ref.shape[1], new_ref.shape[1]
    rope = pe_ref.shape[1]
    pick = lax.broadcasted_iota(jnp.int32, (rows, count), 0) - lax.broadcasted_iota(jnp.int32, (rows, count), 1) == length
    picked = dot_nn(pick.astype(F32).astype(BF16), new_ref[0])
    shift = lax.broadcasted_iota(jnp.int32, (rows, kv_rank), 0) - length
    lat_out[0] = jnp.where(jnp.logical_and(shift >= 0, shift < count), picked[:, :kv_rank], lat_ref[0].astype(F32)).astype(BF16)
    picked_pe = picked[:, kv_rank:].T[:rope]
    shift = lax.broadcasted_iota(jnp.int32, (rope, rows), 1) - length
    pe_out[0] = jnp.where(jnp.logical_and(shift >= 0, shift < count), picked_pe, pe_ref[0].astype(F32)).astype(BF16)
    y_out[...] = y_ref[...]


def update_caches(length, lat, pe, gath_kv, block_out):
    def spec(shape):
        return pl.BlockSpec((1,) + shape[1:], lambda b, length: (b, 0, 0))

    shapes = [lat.shape, pe.shape, gath_kv.shape, block_out.shape]
    return pl.pallas_call(
        functools.partial(cache_kernel, lat.shape[2]),
        out_shape=tuple(jax.ShapeDtypeStruct(shape, BF16) for shape in (lat.shape, pe.shape, block_out.shape)),
        grid_spec=pltpu.PrefetchScalarGridSpec(
            num_scalar_prefetch=1, grid=(lat.shape[0],),
            in_specs=[spec(shape) for shape in shapes],
            out_specs=[spec(shape) for shape in (lat.shape, pe.shape, block_out.shape)],
        ),
        compiler_params=pltpu.CompilerParams(vmem_limit_bytes=67_000_000),
        name="write_caches",
    )(length, lat, pe, gath_kv, block_out)


def solution(mesh):
    tp = mesh.shape["tp"]

    def local_step(hidden, lengths, rope_cos, rope_sin, cache_lat, cache_pe, norm_in, w_dq, norm_q, w_dkv, norm_kv, w_uq, w_uk, w_uv, w_out):
        pe_t = jnp.transpose(cache_pe, (0, 2, 1))
        block_out, gath_kv = attention_block(
            tp, lengths, hidden, jnp.transpose(rope_cos, (0, 2, 1)), jnp.transpose(rope_sin, (0, 2, 1)), cache_lat, pe_t,
            norm_in, w_dq, norm_q, w_dkv.T, norm_kv, jnp.transpose(w_uq, (1, 2, 0)), w_uk, w_uv, w_out)
        lat_all, pe_all_t, block_out = update_caches(lengths, cache_lat, pe_t, gath_kv, block_out)
        return block_out, lat_all, jnp.transpose(pe_all_t, (0, 2, 1))

    spec_tok = P("dp", "tp", None)
    spec_len = P("dp")
    spec_seq = P("dp", None, None)
    spec_vec = P(None)
    spec_mat = P(None, None)
    spec_head = P(None, "tp", None)
    spec_rows = P("tp", None)
    in_specs = (spec_tok, spec_len, spec_seq, spec_seq, spec_seq, spec_seq, spec_vec, spec_mat, spec_vec, spec_mat, spec_vec, spec_head, spec_head, spec_head, spec_rows)
    return jax.shard_map(local_step, mesh=mesh, in_specs=in_specs, out_specs=(spec_tok, spec_seq, spec_seq), check_vma=False)
```

time: 962 us -> 271 us (0.28)
  matrix products: 390 us -> 0 us
  waiting for transfers between devices: 342 us -> 0 us
  Pallas kernels: 0 us -> 270 us
  local copies, waits for them, and re-layouts: 111 us -> 0 us
  other arithmetic: 95.6 us -> 0 us
  between operations: 14.7 us -> 0.64 us
    dot_general x7 -> x0, matrix products: 289 us -> none  [the longest x1 56.9 us: local_step(): jnp.einsum('bthv,hvd->btd', attn_out, out_heads, preferred_element_type=j...]
    pallas_call x0 -> x2, Pallas kernels: none -> 270 us  [the longest x1 258 us: attention_block(): pl.pallas_call(functools.partial(main_kernel, dm, INPUTS + OUTPUTS + tupl...]
    reduce_scatter x1 -> x0, waiting for transfers between devices: 231 us -> none  [local_step(): reduced = lax.psum_scatter(head_sum, 'tp', scatter_dimension=1, tiled=True)]
    all_gather x1 -> x0, waiting for transfers between devices: 110 us -> none  [local_step(): gathered = lax.all_gather(hidden, 'tp', axis=1, tiled=True)]
    sub x1 -> x0, matrix products: 102 us -> none  [local_step(): attn_probs = jax.nn.softmax(scores, axis=-1).astype(jnp.bfloat16)]
    scatter x25 -> x0, other arithmetic: 67 us -> none
    scatter x48 -> x0, local copies, waits for them, and re-layouts: 53.4 us -> none
    dot_general x1 -> x0, local copies, waits for them, and re-layouts: 50.2 us -> none  [local_step(): jnp.einsum('bsc,chv->bshv', lat_all, w_uv, preferred_element_type=jnp.flo...]
  transfers between devices with their start and end apart: 2 -> 0, of which waited for: 2 -> 0; matrix products, arithmetic and copies ran while one was open for 0% -> 0% of each run, Pallas kernels for 0% -> 0%
where the time goes in v2:
time: 271 us
  Pallas kernels  270 us (100%)
    pallas_call x1, Pallas kernels, attention_block(): pl.pallas_call(functools.partial(main_kernel, dm, INPUTS + OUTPUTS + tupl...  258 us
    pallas_call x1, Pallas kernels, update_caches(): pl.pallas_call(functools.partial(cache_kernel, lat.shape[2]), out_shape=t...  11.6 us

profile of v2, /device:TPU:112, one launch (start us, length us, event | category | flops | bytes accessed | tf_op | source)
XLA Modules:
  0.0 270.6 jit_solution(8083363119435717291)
XLA Ops:
  0.6 258.3 %attend_project.1 = (bf16[6,48,5120]{2,1,0:T(8,128)(2,1)}, bf16[6,384,1536]{2,1,0:T(8,128)(2,1)}, bf16[6,384,640]{2,1,0:T(8,128)(2,1)}) custom-call(s32[6]{0:T(128)} %len_ref.1, bf16[6,48,5120]{2,1,0:T(8,128)(2,1)} %refs_1_.1, f32[6,32,384]{2,1,0:T(8,128)} %bitcast.10, f32[6,32,384]{2,1,0:T(8,128)} %bitcast.11, bf16[6,896,512]{2,1,0:T(8,128)(2,1)} %lat_ref.1, ...), custom_call_target="tpu_custom_call" | custom-call | tf_op jit(solution)/shard_map/attend_project/pallas_call | solution.py:671
  259.0 11.6 %write_caches.1 = (bf16[6,896,512]{2,1,0:T(8,128)(2,1)}, bf16[6,64,896]{2,1,0:T(8,128)(2,1)}, bf16[6,48,5120]{2,1,0:T(8,128)(2,1)}) custom-call(s32[6]{0:T(128)} %len_ref.1, bf16[6,896,512]{2,1,0:T(8,128)(2,1)} %lat_ref.1, bf16[6,64,896]{2,1,0:T(8,128)(2,1)} %bitcast.9, bf16[6,384,640]{2,1,0:T(8,128)(2,1)} %get-tuple-element.8.new_ref, ...), custom_call_target="tpu_custom_call" | custom-call | tf_op jit(solution)/shard_map/write_caches/pallas_call | solution.py:706
